TPU v7x, 32 devices: a whole 2x2x4 slice. The times are simulated.
32 devices in a mesh: seq: 8 (over y, x, core), rep: 4 (over z).
Axes of the slice: x: 2, y: 2, z: 4, core: 2. Of those that a mesh axis runs over, the one named last changes fastest.
Arguments:
- queries: bfloat16 [4096, 2048], P(('rep', 'seq')), parts along dimension 0, may hold values from -6 to 6
- keys: bfloat16 [4096, 2048], P(('rep', 'seq')), parts along dimension 0, may hold values from -6 to 6
- values: bfloat16 [4096, 2048], P(('rep', 'seq')), parts along dimension 0, may hold values from -6 to 6
- short_taps: float32 [3, 3, 2048], replicated, may hold values from -3.5 to 3.5
- decay: float32 [2048, 16], replicated, may hold values from 0.00048828125 to 0.1
- residue: float32 [2048, 16], replicated, may hold values from -1.5 to 1.5
- skip: float32 [2048], replicated, may hold values from -3 to 3
- w_out: bfloat16 [2048, 2048], replicated, may hold values from -0.125 to 0.125
Outputs:
- layer_out: bfloat16 [4096, 2048], P(('rep', 'seq')), parts along dimension 0
There are 4 independent parts, one for each index of `rep`. A program takes and returns all parts, laid end to end along the dimension named above; an argument that names none is the same for every part. Nothing has to cross between parts.
All inputs are finite; a program needn't handle non-finite values.
Results may differ from a plain program's by a relative error of at most 0.014.
Values may be sent and summed in bfloat16 or wider, within the bound.
A program may use at most 64 MiB of HBM per device.

v0:
```python
import math

import jax
import jax.numpy as jnp
from jax import lax
from jax.sharding import PartitionSpec as P


def passed_along(value, axis, by):
    devices = lax.axis_size(axis)
    pairs = [(i, i + by) for i in range(devices) if 0 <= i + by < devices]
    return lax.ppermute(value, axis, pairs)


def short_conv(tokens, before, taps):
    extended = jnp.concatenate([before, tokens], axis=0).astype(jnp.float32)
    result = taps[0] * extended[2:] + taps[1] * extended[1:-1]
    return result + taps[2] * extended[:-2]


def modal_local(sig_t, rates, weights):
    chans, length = sig_t.shape
    blk_rows = math.gcd(length, 128)
    blk_count = length // blk_rows
    group = math.gcd(chans, 128)
    groups = chans // group
    modes = rates.shape[1]
    places = jnp.arange(blk_rows, dtype=jnp.float32)
    row_idx = jnp.arange(blk_rows, dtype=jnp.int32)
    lower = row_idx[:, None] >= row_idx[None, :]

    def within(items):
        piece, grp_rates, grp_weights = items
        falling = jnp.exp(-places[None, None, :] * grp_rates[:, :, None])
        rising = jnp.exp(places[None, None, :] * grp_rates[:, :, None]) * grp_weights[:, :, None]
        toeplitz = jnp.einsum("gmi,gmj->gij", falling, rising, precision=lax.Precision.HIGHEST)
        toeplitz = jnp.where(lower[None], toeplitz, 0.0)
        inner = jnp.einsum("gij,gbj->gbi", toeplitz, piece, precision=lax.Precision.HIGHEST)
        end_table = jnp.exp(-(blk_rows - 1.0 - places)[None, None, :] * grp_rates[:, :, None])
        ending = jnp.einsum("gmj,gbj->gmb", end_table, piece, precision=lax.Precision.HIGHEST)
        return (inner, ending)

    grouped = sig_t.reshape(groups, group, blk_count, blk_rows)
    rate_groups = rates.reshape(groups, group, modes)
    weight_groups = weights.reshape(groups, group, modes)
    inner, ending = lax.map(within, (grouped, rate_groups, weight_groups))
    inner = inner.reshape(chans, blk_count, blk_rows)
    ending = ending.reshape(chans, modes, blk_count)
    blk_idx = jnp.arange(blk_count, dtype=jnp.int32)
    gaps = (blk_idx[:, None] - blk_idx[None, :]).astype(jnp.float32)
    earlier_mask = gaps >= 0.0
    clamped = jnp.maximum(gaps, 0.0)

    def carry_mode(items):
        rate_col, end_rows = items
        linking = jnp.exp(-blk_rows * rate_col[:, None, None] * clamped[None])
        linking = jnp.where(earlier_mask[None], linking, 0.0)
        return jnp.einsum("cij,cj->ci", linking, end_rows, precision=lax.Precision.HIGHEST)

    reached = lax.map(carry_mode, (rates.T, ending.transpose(1, 0, 2)))
    reached = reached.transpose(1, 0, 2)
    return (inner, reached)


def modal_finish(inner, reached, start_state, rates, weights):
    chans, blk_count, blk_rows = inner.shape
    places = jnp.arange(blk_rows, dtype=jnp.float32)
    blk_places = jnp.arange(blk_count, dtype=jnp.float32)
    entering = jnp.concatenate(
        [jnp.zeros((chans, reached.shape[1], 1), jnp.float32), reached[:, :, :-1]], axis=2
    )
    entering = (
        entering
        + jnp.exp(-blk_rows * blk_places[None, None, :] * rates[:, :, None])
        * start_state[:, :, None]
    )
    carry_table = jnp.exp(-(places + 1.0)[None, None, :] * rates[:, :, None]) * weights[:, :, None]
    carried = jnp.einsum("cmi,cmb->cbi", carry_table, entering, precision=lax.Precision.HIGHEST)
    return (inner + carried).reshape(chans, blk_count * blk_rows)


def body(queries, keys, values, short_taps, decay, residue, skip, w_out):
    tok_rows = queries.shape[0]
    tails = jnp.stack([queries[tok_rows - 2 :], keys[tok_rows - 2 :], values[tok_rows - 2 :]])
    before = passed_along(tails, "seq", 1)
    q_short = short_conv(queries, before[0], short_taps[0])
    k_short = short_conv(keys, before[1], short_taps[1])
    v_short = short_conv(values, before[2], short_taps[2])
    mixed_in = (k_short * v_short).astype(jnp.bfloat16)
    weights = residue * jnp.sqrt(1.0 - jnp.exp(-2.0 * decay))
    mixed_t = mixed_in.T
    chans = decay.shape[0] // lax.axis_size("seq")
    spread = lax.all_to_all(mixed_t, "seq", split_axis=0, concat_axis=1, tiled=True)
    first_chan = lax.axis_index("seq") * chans
    rates_mine = lax.dynamic_slice_in_dim(decay, first_chan, chans, 0)
    weights_mine = lax.dynamic_slice_in_dim(weights, first_chan, chans, 0)
    skip_mine = lax.dynamic_slice_in_dim(skip, first_chan, chans, 0)
    signal = spread.astype(jnp.float32)
    inner, reached = modal_local(signal, rates_mine, weights_mine)
    convolved = modal_finish(inner, reached, jnp.zeros_like(rates_mine), rates_mine, weights_mine)
    long_part = (convolved + skip_mine[:, None] * signal).astype(jnp.bfloat16)
    long_t = lax.all_to_all(long_part, "seq", split_axis=1, concat_axis=0, tiled=True)
    long_out = long_t.T
    gated = (q_short * long_out.astype(jnp.float32)).astype(jnp.bfloat16)
    return jnp.dot(gated, w_out, preferred_element_type=jnp.float32).astype(jnp.bfloat16)


def solution(mesh):
    placed = (
        P(("rep", "seq"), None),
        P(("rep", "seq"), None),
        P(("rep", "seq"), None),
        P(),
        P(),
        P(),
        P(),
        P(),
    )
    return jax.shard_map(
        body, mesh=mesh, in_specs=placed, out_specs=P(("rep", "seq"), None), check_vma=False
    )
```

profile of v0, /device:TPU:0, one launch (start us, length us, event | category | flops | bytes accessed | tf_op | source)
XLA Modules:
  0.0 131.7 jit_solution(10662076295898209683)
XLA Ops:
  0.0 0.8 slice_bitcast_fusion.2
  0.8 0.8 slice_bitcast_fusion
  1.6 2.4 %collective-permute-start = (bf16[3,2,2048]{2,1,0:T(2,128)(2,1)S(1)}, bf16[3,2,2048]{2,1,0:T(2,128)(2,1)S(1)}, u32[]{:S(2)}, u32[]{:S(2)}) collective-permute-start(bf16[3,2,2048]{2,1,0:T(2,128)(2,1)S(1)} %pad_maximum_fusion), channel_id=1, source_target_pairs={{0,4},{4,8},{8,12},{12,16},{16,20},{20,24},{24,28},{1,5},{5,9},{9,... | collective-permute-start | bytes 73736 | tf_op jit(solution)/shard_map/ppermute | solution.py:12
  4.0 1.1 fusion.68
  5.1 1.3 copy.32
  6.4 1.3 copy.34
  9.2 3.7 %fusion.57 = bf16[128,2048]{0,1:T(8,128)(2,1)} fusion(f32[130,2048]{0,1:T(8,128)S(1)} %maximum_convert_fusion.2, f32[130,2048]{0,1:T(8,128)S(1)} %maximum_convert_fusion.1, f32[2048]{0:T(1024)S(1)} %bitcast.110, f32[2048]{0:T(1024)S(1)} %bitcast.111, f32[2048]{0:T(1024)S(1)} %bitcast.107, f32[2048]{0:T(1024)S(1)} %bitcast.108, f32[2048]{0:T(1024)S(1)} %bitcast.109, ...), kind=kLoop, calls=%fused_computation.57 | loop fusion | flops 3145728 | bytes 6864896 | tf_op jit(solution)/shard_map/convert_element_type | solution.py:89
  13.0 5.0 %all-to-all-start = ((bf16[8,256,128]{2,1,0:T(8,128)(2,1)}), bf16[8,256,128]{2,1,0:T(8,128)(2,1)S(1)}, u32[]{:S(2)}, u32[]{:S(2)}) async-start(bf16[8,256,128]{2,1,0:T(8,128)(2,1)} %bitcast.17), calls=%async_computation | async-start | bytes 1048576 | tf_op jit(solution)/shard_map/all_to_all | solution.py:93
  18.0 0.8 dynamic-slice_multiply_fusion.1
  18.9 0.8 dynamic_slice.33
  19.7 7.9 %all-to-all-done = bf16[8,256,128]{2,1,0:T(8,128)(2,1)S(1)} async-done(((bf16[8,256,128]{2,1,0:T(8,128)(2,1)}), bf16[8,256,128]{2,1,0:T(8,128)(2,1)S(1)}, u32[]{:S(2)}, u32[]{:S(2)}) %all-to-all-start) | async-done | bytes 524320 | tf_op jit(solution)/shard_map/all_to_all | solution.py:93
  28.0 60.6 %while.27 = (s32[]{:T(128)}, f32[2,128,8,128]{3,2,1,0:T(8,128)}, f32[2,128,16,8]{2,3,1,0:T(8,128)S(1)}, f32[2,128,8,128]{3,2,1,0:T(8,128)S(1)}, f32[2,128,16]{2,...) while((s32[]{:T(128)}, f32[2,128,8,128]{3,2,1,0:T(8,128)}, ...), condition=%wide.region_1.2_spmd.clone.clone, body=%wide.region_0.1_spmd.clone.clone.sunk | while | flops 632308096 | bytes 27414664 | solution.py:46
  28.2 14.0 %fusion.89 = f32[128,128,128]{2,1,0:T(8,128)S(1)} fusion(f32[128,16]{1,0:T(8,128)S(1)} %get-tuple-element.274, f32[128,16]{1,0:T(8,128)S(1)} %get-tuple-element.275, f32[128]{0:T(128)S(1)} %negate_bitcast_fusion.2), kind=kOutput, calls=%fused_computation.16.clone.1 | convolution fusion | flops 403439616 | bytes 8405504 | tf_op jit(solution)/shard_map/while/body/eval_jaxpr/gmi,gmj->gij/dot_general | solution.py:36
  42.3 13.1 %fusion.90 = f32[2,128,8,128]{3,2,1,0:T(8,128)S(1)} fusion(f32[2,128,8,128]{3,2,1,0:T(8,128)S(1)} %copy-done.1, s32[]{:T(128)} %get-tuple-element.283, f32[128,128,128]{2,1,0:T(8,128)S(1)} %fusion.89, pred[128,128]{1,0:T(8,128)(4,1)S(1)} %iota_compare_fusion.2, f32[2,128,8,128]{3,2,1,0:T(8,128)S(1)} %get-tuple-element.293), kind=kOutput, calls=%fused_computation.10.clone.1 | convolution fusion | flops 203423744 | bytes 9454592 | tf_op jit(solution)/shard_map/while/body/eval_jaxpr/gij,gbj->gbi/dot_general | solution.py:38
  55.4 1.0 copy-done.2
  56.4 1.9 %fusion.92 = f32[2,128,16,8]{2,3,1,0:T(8,128)S(1)} fusion(f32[2,128,16,8]{2,3,1,0:T(8,128)S(1)} %get-tuple-element.285, s32[]{:T(128)} %get-tuple-element.283, f32[128]{0:T(128)S(1)} %fusion.91, f32[128,16]{1,0:T(8,128)S(1)} %get-tuple-element.275, f32[2,128,8,128]{3,2,1,0:T(8,128)S(1)} %get-tuple-element.293), kind=kOutput, calls=%fused_computation.12.clone.1 | convolution fusion | flops 25427968 | bytes 1115648 | tf_op jit(solution)/shard_map/while/body/eval_jaxpr/gmj,gbj->gmb/dot_general | solution.py:40
  58.3 14.0 %fusion.89 = f32[128,128,128]{2,1,0:T(8,128)S(1)} fusion(f32[128,16]{1,0:T(8,128)S(1)} %get-tuple-element.274, f32[128,16]{1,0:T(8,128)S(1)} %get-tuple-element.275, f32[128]{0:T(128)S(1)} %negate_bitcast_fusion.2), kind=kOutput, calls=%fused_computation.16.clone.1 | convolution fusion | flops 403439616 | bytes 8405504 | tf_op jit(solution)/shard_map/while/body/eval_jaxpr/gmi,gmj->gij/dot_general | solution.py:36
  72.4 13.1 %fusion.90 = f32[2,128,8,128]{3,2,1,0:T(8,128)S(1)} fusion(f32[2,128,8,128]{3,2,1,0:T(8,128)S(1)} %copy-done.1, s32[]{:T(128)} %get-tuple-element.283, f32[128,128,128]{2,1,0:T(8,128)S(1)} %fusion.89, pred[128,128]{1,0:T(8,128)(4,1)S(1)} %iota_compare_fusion.2, f32[2,128,8,128]{3,2,1,0:T(8,128)S(1)} %get-tuple-element.293), kind=kOutput, calls=%fused_computation.10.clone.1 | convolution fusion | flops 203423744 | bytes 9454592 | tf_op jit(solution)/shard_map/while/body/eval_jaxpr/gij,gbj->gbi/dot_general | solution.py:38
  85.6 1.0 copy-done.2
  86.5 1.9 %fusion.92 = f32[2,128,16,8]{2,3,1,0:T(8,128)S(1)} fusion(f32[2,128,16,8]{2,3,1,0:T(8,128)S(1)} %get-tuple-element.285, s32[]{:T(128)} %get-tuple-element.283, f32[128]{0:T(128)S(1)} %fusion.91, f32[128,16]{1,0:T(8,128)S(1)} %get-tuple-element.275, f32[2,128,8,128]{3,2,1,0:T(8,128)S(1)} %get-tuple-element.293), kind=kOutput, calls=%fused_computation.12.clone.1 | convolution fusion | flops 25427968 | bytes 1115648 | tf_op jit(solution)/shard_map/while/body/eval_jaxpr/gmj,gbj->gmb/dot_general | solution.py:40
  89.0 14.5 %while.26 = (s32[]{:T(128)}, f32[16,256,8]{1,2,0:T(8,128)S(1)}, f32[16,256]{1,0:T(8,128)S(1)}, f32[16,256,8]{1,2,0:T(8,128)S(1)}, s32[]{:T(128)}) while((s32[]{:T(128)}, f32[16,256,8]{1,2,0:T(8,128)S(1)}, f32[16,256]{1,0:T(8,128)S(1)}, f32[16,256,8]{1,2,0:T(8,128)S(1)}, s32[]{:T(128)}) %tuple.69), condition=%wide.region_3.4_spmd.clone, body=%wide.region_2.3_spmd.clone.sunk | while | flops 64130 | bytes 85705 | solution.py:60
  89.2 0.6 multiply_reduce_fusion.2
  90.1 0.6 multiply_reduce_fusion.2
  96.4 0.6 multiply_reduce_fusion.2
  97.3 0.6 multiply_reduce_fusion.2
  98.2 0.6 multiply_reduce_fusion.2
  104.0 4.9 %fusion.52 = bf16[256,8,128]{2,1,0:T(8,128)(2,1)S(1)} fusion(f32[256,8,128]{2,1,0:T(8,128)S(1)} %bitcast.112, f32[256,16,8]{1,2,0:T(8,128)S(1)} %copy.41, f32[256,16]{1,0:T(8,128)S(1)} %bitcast.96, f32[256,16]{1,0:T(8,128)S(1)} %bitcast.94, f32[128]{0:T(128)S(1)} %add_negate_fusion, f32[256]{0:T(256)S(1)} %dynamic_slice.33, ...), kind=kOutput, calls=%fused_computation.53 | convolution fusion | flops 52690944 | bytes 2262528 | tf_op jit(solution)/shard_map/cmi,cmb->cbi/dot_general | solution.py:78
  108.9 0.9 copy.42
  109.8 4.1 %all-to-all-start.1 = ((bf16[256,8,128]{2,0,1:T(8,128)(2,1)}), bf16[256,8,128]{2,0,1:T(8,128)(2,1)}, u32[]{:S(2)}, u32[]{:S(2)}) async-start(bf16[256,8,128]{2,0,1:T(8,128)(2,1)} %copy.42), calls=%async_computation.1 | async-start | bytes 1048576 | tf_op jit(solution)/shard_map/all_to_all | solution.py:102
  115.0 8.7 %all-to-all-done.1 = bf16[256,8,128]{2,0,1:T(8,128)(2,1)} async-done(((bf16[256,8,128]{2,0,1:T(8,128)(2,1)}), bf16[256,8,128]{2,0,1:T(8,128)(2,1)}, u32[]{:S(2)}, u32[]{:S(2)}) %all-to-all-start.1) | async-done | bytes 524320 | tf_op jit(solution)/shard_map/all_to_all | solution.py:102
  123.7 2.5 %fusion.63 = bf16[128,2048]{0,1:T(8,128)(2,1)S(1)} fusion(f32[130,2048]{0,1:T(8,128)S(1)} %maximum_convert_fusion, f32[2048]{0:T(1024)S(1)} %bitcast.103, f32[2048]{0:T(1024)S(1)} %bitcast.104, f32[2048]{0:T(1024)S(1)} %bitcast.105, bf16[256,8,128]{2,0,1:T(8,128)(2,1)} %all-to-all-done.1), kind=kLoop, calls=%fused_computation.69 | loop fusion | flops 2097152 | bytes 4218880 | tf_op jit(solution)/shard_map/convert_element_type | solution.py:104
  126.2 5.5 %convolution_convert_fusion = bf16[128,2048]{1,0:T(8,128)(2,1)} fusion(bf16[128,2048]{0,1:T(8,128)(2,1)S(1)} %fusion.63, bf16[2048,2048]{1,0:T(8,128)(2,1)} %param.19), kind=kOutput, calls=%fused_computation.46 | convolution fusion | flops 1074003968 | bytes 9437184 | tf_op jit(solution)/shard_map/dot_general | solution.py:105
  (162 shorter events, 14.7 us)
Async XLA Ops:
  1.6 6.1 %collective-permute-start = (bf16[3,2,2048]{2,1,0:T(2,128)(2,1)S(1)}, bf16[3,2,2048]{2,1,0:T(2,128)(2,1)S(1)}, u32[]{:S(2)}, u32[]{:S(2)}) collective-permute-start(bf16[3,2,2048]{2,1,0:T(2,128)(2,1)S(1)} %pad_maximum_fusion), channel_id=1, source_target_pairs={{0,4},{4,8},{8,12},{12,16},{16,20},{20,24},{24,28},{1,5},{5,9},{9,... | collective-permute-start | bytes 73736 | tf_op jit(solution)/shard_map/ppermute | solution.py:12
  13.0 14.7 %all-to-all-start = ((bf16[8,256,128]{2,1,0:T(8,128)(2,1)}), bf16[8,256,128]{2,1,0:T(8,128)(2,1)S(1)}, u32[]{:S(2)}, u32[]{:S(2)}) async-start(bf16[8,256,128]{2,1,0:T(8,128)(2,1)} %bitcast.17), calls=%async_computation | async-start | bytes 1048576 | tf_op jit(solution)/shard_map/all_to_all | solution.py:93
  28.2 14.1 %copy-start.1 = (f32[2,128,8,128]{3,2,1,0:T(8,128)S(1)}, f32[2,128,8,128]{3,2,1,0:T(8,128)}, u32[]{:S(2)}) copy-start(f32[2,128,8,128]{3,2,1,0:T(8,128)} %get-tuple-element.284) | copy-start | bytes 3145732 | tf_op jit(solution)/shard_map/while
  55.4 1.0 copy-start.2
  58.3 14.1 %copy-start.1 = (f32[2,128,8,128]{3,2,1,0:T(8,128)S(1)}, f32[2,128,8,128]{3,2,1,0:T(8,128)}, u32[]{:S(2)}) copy-start(f32[2,128,8,128]{3,2,1,0:T(8,128)} %get-tuple-element.284) | copy-start | bytes 3145732 | tf_op jit(solution)/shard_map/while
  85.5 1.0 copy-start.2
  89.0 15.0 %copy-start.3 = (f32[2,128,8,128]{3,2,1,0:T(8,128)S(1)}, f32[2,128,8,128]{3,2,1,0:T(8,128)}, u32[]{:S(2)}) copy-start(f32[2,128,8,128]{3,2,1,0:T(8,128)} %get-tuple-element.120) | copy-start | bytes 3145732
  108.9 5.0 %copy-start = (bf16[128,2048]{1,0:T(8,128)(2,1)S(1)}, bf16[128,2048]{1,0:T(8,128)(2,1)}, u32[]{:S(2)}) copy-start(bf16[128,2048]{1,0:T(8,128)(2,1)} %param.12) | copy-start | bytes 1572868
  109.8 13.9 %all-to-all-start.1 = ((bf16[256,8,128]{2,0,1:T(8,128)(2,1)}), bf16[256,8,128]{2,0,1:T(8,128)(2,1)}, u32[]{:S(2)}, u32[]{:S(2)}) async-start(bf16[256,8,128]{2,0,1:T(8,128)(2,1)} %copy.42), calls=%async_computation.1 | async-start | bytes 1048576 | tf_op jit(solution)/shard_map/all_to_all | solution.py:102
where the time goes:
time: 132 us
  matrix products  68.4 us (52%)
  other arithmetic  19.4 us (15%)
  waiting for transfers between devices  16.6 us (13%)
  local copies, waits for them, and re-layouts  14.2 us (11%)
  starting transfers between devices  11.5 us (9%)
    dot_general x2, matrix products, within(): jnp.einsum('gmi,gmj->gij', falling, rising, precision=lax.Precision.HIGHEST)  28.1 us
    dot_general x2, matrix products, within(): jnp.einsum('gij,gbj->gbi', toeplitz, piece, precision=lax.Precision.HIGHEST)  26.2 us
    while x16, other arithmetic  10.2 us
    all_to_all x1, waiting for transfers between devices, body(): lax.all_to_all(long_part, 'seq', split_axis=1, concat_axis=0, tiled=True)  8.69 us
    all_to_all x1, waiting for transfers between devices, body(): lax.all_to_all(mixed_t, 'seq', split_axis=0, concat_axis=1, tiled=True)  7.95 us
    dot_general x1, matrix products, body(): jnp.dot(gated, w_out, preferred_element_type=jnp.float32)  5.47 us
    all_to_all x1, starting transfers between devices, body(): lax.all_to_all(mixed_t, 'seq', split_axis=0, concat_axis=1, tiled=True)  4.99 us
    dot_general x1, matrix products, modal_finish(): jnp.einsum('cmi,cmb->cbi', carry_table, entering, precision=lax.Precision...  4.9 us
  transfers between devices with their start and end apart: 3, of which 2 were waited for; matrix products, arithmetic and copies ran while one was open for 5% of the time, Pallas kernels for 0%

commit v1 on v0

v1 whole, which is shorter than its diff:
```python
import functools
import math

import jax
import jax.numpy as jnp
from jax import lax
from jax.experimental import pallas as pl
from jax.experimental.pallas import tpu as pltpu
from jax.sharding import PartitionSpec as P

MESH = pl.DeviceIdType.MESH
F32 = jnp.float32
SUB = 8


def kernel(
    n, width,
    q_hbm, k_hbm, v_hbm, taps_ref, rates_ref, residue_ref, skip_ref, w_hbm,
    out_ref,
    q_in, k_in, v_in, w_in, tails_out, tails_in, ext, sig, q_short, partial, states,
    carry_table, tap_table, gated, ends, before, totals, earlier, total_out,
    in_sems, w_sem, tail_sems, pair_send, pair_recv, group_send, group_recv,
):
    rows, chans = q_in.shape
    modes = rates_ref.shape[0]
    blocks = rows // SUB
    chunks = chans // width
    groups = n // 2
    me = lax.axis_index("seq")
    group = lax.div(me, 2)
    odd = lax.rem(me, 2)

    barrier = pltpu.get_barrier_semaphore()

    def greet(step, carry):
        pl.semaphore_signal(
            barrier, inc=1, device_id={"seq": lax.rem(me + step, n)}, device_id_type=MESH
        )
        return carry

    lax.fori_loop(1, n, greet, 0)
    loads = [
        pltpu.make_async_copy(src, dst, in_sems.at[i])
        for i, (src, dst) in enumerate(((q_hbm, q_in), (k_hbm, k_in), (v_hbm, v_in)))
    ]
    for load in loads:
        load.start()
    w_load = pltpu.make_async_copy(w_hbm, w_in, w_sem)
    w_load.start()

    for load in loads:
        load.wait()
    for i, tokens in enumerate((q_in, k_in, v_in)):
        last = tokens[rows - 16 :, :].astype(F32)
        tails_out[2 * i : 2 * i + 2, :] = last[14:16]
    tails_out[6:8, :] = jnp.zeros((2, chans), F32)
    pl.semaphore_wait(barrier, n - 1)

    def tail_copy():
        return pltpu.make_async_remote_copy(
            src_ref=tails_out, dst_ref=tails_in, send_sem=tail_sems.at[0], recv_sem=tail_sems.at[1],
            device_id={"seq": lax.rem(me + 1, n)}, device_id_type=MESH,
        )

    def pair_copy(g):
        return pltpu.make_async_remote_copy(
            src_ref=ends.at[g], dst_ref=before.at[g], send_sem=pair_send.at[g], recv_sem=pair_recv.at[g],
            device_id={"seq": me + 1 - 2 * odd}, device_id_type=MESH,
        )

    def group_copy(source, target, core, g):
        return pltpu.make_async_remote_copy(
            src_ref=totals.at[g], dst_ref=earlier.at[source, g],
            send_sem=group_send.at[target, core, g], recv_sem=group_recv.at[source, g],
            device_id={"seq": 2 * target + core}, device_id_type=MESH,
        )

    @pl.when(me < n - 1)
    def _():
        tail_copy().start()

    @pl.when(me == 0)
    def _():
        tails_in[...] = jnp.zeros_like(tails_in)

    @pl.when(odd == 0)
    def _():
        before[...] = jnp.zeros_like(before)

    place = lax.broadcasted_iota(jnp.int32, (SUB, width), 0)
    steps = (place + 1).astype(F32)

    def tables(g, carry):
        cols = pl.ds(pl.multiple_of(g * width, width), width)
        rates = rates_ref[:, cols]
        weights = residue_ref[:, cols] * jnp.sqrt(1.0 - jnp.exp(-2.0 * rates))
        total = jnp.zeros((SUB, width), F32)
        for m in range(modes):
            row = jnp.exp(-rates[m : m + 1] * steps) * weights[m : m + 1]
            carry_table[m * SUB : (m + 1) * SUB, cols] = row
            total = total + row
        first = jnp.sum(weights, axis=0, keepdims=True) + skip_ref[:, cols]
        taps = jnp.where(place == 0, first, pltpu.roll(total, 1, 0))
        for s in range(SUB):
            shifted = taps if s == 0 else jnp.where(place >= s, pltpu.roll(taps, s, 0), 0.0)
            tap_table[s * SUB : (s + 1) * SUB, cols] = shifted
        return carry

    lax.fori_loop(0, chunks, tables, 0)

    @pl.when(me > 0)
    def _():
        tail_copy().wait_recv()

    def combine(g):
        @pl.when(odd == 1)
        def _():
            pair_copy(g).wait_recv()

            @pl.when(group < groups - 1)
            def _():
                cols = pl.ds(pl.multiple_of(g * width, width), width)
                span = jnp.exp(-float(rows) * rates_ref[:, cols])
                totals[g] = span * before[g] + ends[g]

                def send(target, carry):
                    for core in range(2):
                        group_copy(group, target, core, g).start()
                    return carry

                lax.fori_loop(group + 1, groups, send, 0)

    strip = math.gcd(rows, 16)

    def local(g, carry):
        cols = pl.ds(pl.multiple_of(g * width, width), width)
        for i, tokens in enumerate((q_in, k_in, v_in)):
            ext[i, SUB - 2 : SUB, :] = tails_in[2 * i : 2 * i + 2, cols]
            for r in range(0, rows, strip):
                ext[i, SUB + r : SUB + r + strip, :] = tokens[r : r + strip, cols].astype(F32)

        def short(i, r):
            result = taps_ref[i, 0:1, cols] * ext[i, SUB + r : SUB + r + strip, :]
            result = result + taps_ref[i, 1:2, cols] * ext[i, SUB + r - 1 : SUB + r + strip - 1, :]
            return result + taps_ref[i, 2:3, cols] * ext[i, SUB + r - 2 : SUB + r + strip - 2, :]

        for r in range(0, rows, strip):
            mixed = (short(1, r) * short(2, r)).astype(jnp.bfloat16)
            sig[r : r + strip, :] = mixed.astype(F32)
            q_short[r : r + strip, cols] = short(0, r)

        fade = jnp.exp(-rates_ref[:, cols])

        def block(b, state):
            states[pl.ds(pl.multiple_of(b * modes, modes), modes), cols] = state
            base = pl.multiple_of(b * SUB, SUB)
            acc = None
            for s in range(SUB):
                row = sig[pl.ds(base + s, 1), :]
                state = state * fade + row
                term = tap_table[s * SUB : (s + 1) * SUB, cols] * row
                acc = term if acc is None else acc + term
            partial[pl.ds(base, SUB), cols] = acc
            return state

        ends[g] = lax.fori_loop(0, blocks, block, jnp.zeros((modes, width), F32), unroll=2)

        @pl.when(odd == 0)
        def _():
            pair_copy(g).start()

        @pl.when(g > 0)
        def _():
            combine(g - 1)

        return carry

    lax.fori_loop(0, chunks, local, 0)
    combine(chunks - 1)
    w_load.wait()
    batch = 4 if blocks % 4 == 0 else 1
    tile = math.gcd(chans, 512)

    def finish(g, carry):
        cols = pl.ds(pl.multiple_of(g * width, width), width)
        rates = rates_ref[:, cols]
        far = jnp.exp(-2.0 * rows * rates)

        def gather(source, state):
            group_copy(source, group, odd, g).wait_recv()
            return state * far + earlier[source, g]

        entering = lax.fori_loop(0, group, gather, jnp.zeros((modes, width), F32))
        span = jnp.where(odd == 1, jnp.exp(-float(rows) * rates), 1.0)
        entering = span * entering + before[g]
        fade = jnp.exp(-float(SUB) * rates)
        for b in range(blocks):
            here = slice(b * modes, (b + 1) * modes)
            states[here, cols] = states[here, cols] + entering
            entering = entering * fade

        def outputs(k, inner):
            base = pl.multiple_of(k * batch * SUB, batch * SUB)
            accs = [partial[pl.ds(base + j * SUB, SUB), cols] for j in range(batch)]
            for m in range(modes):
                table = carry_table[m * SUB : (m + 1) * SUB, cols]
                for j in range(batch):
                    row = states[pl.ds((k * batch + j) * modes + m, 1), cols]
                    accs[j] = accs[j] + table * row
            long_out = jnp.concatenate(accs, axis=0).astype(jnp.bfloat16).astype(F32)
            here = pl.ds(base, batch * SUB)
            gated[here, :] = (q_short[here, cols] * long_out).astype(jnp.bfloat16)
            return inner

        lax.fori_loop(0, blocks // batch, outputs, 0)
        for c in range(0, chans, tile):
            piece = jnp.dot(gated[...], w_in[cols, c : c + tile], preferred_element_type=F32)
            total_out[:, c : c + tile] += piece
        return carry

    total_out[...] = jnp.zeros_like(total_out)
    lax.fori_loop(0, chunks, finish, 0)
    out_ref[...] = total_out[...].astype(out_ref.dtype)

    @pl.when(me < n - 1)
    def _():
        tail_copy().wait_send()

    @pl.when(odd == 0)
    def _():
        for g in range(chunks):
            pair_copy(g).wait_send()

    @pl.when(odd == 1)
    def _():
        def sent(target, carry):
            for core in range(2):
                for g in range(chunks):
                    group_copy(group, target, core, g).wait_send()
            return carry

        lax.fori_loop(group + 1, groups, sent, 0)


def solution(mesh):
    n = mesh.shape["seq"]

    def body(queries, keys, values, short_taps, decay, residue, skip, w_out):
        rows, chans = queries.shape
        modes = decay.shape[1]
        width = math.gcd(chans, 512)
        chunks = chans // width
        bf16 = jnp.bfloat16
        vmem = pl.BlockSpec(memory_space=pltpu.VMEM)
        hbm = pl.BlockSpec(memory_space=pl.ANY)
        dma = pltpu.SemaphoreType.DMA
        return pl.pallas_call(
            functools.partial(kernel, n, width),
            out_shape=jax.ShapeDtypeStruct((rows, w_out.shape[1]), bf16),
            in_specs=[hbm, hbm, hbm, vmem, vmem, vmem, vmem, hbm],
            out_specs=vmem,
            scratch_shapes=[
                pltpu.VMEM((rows, chans), bf16),
                pltpu.VMEM((rows, chans), bf16),
                pltpu.VMEM((rows, chans), bf16),
                pltpu.VMEM(w_out.shape, bf16),
                pltpu.VMEM((SUB, chans), F32),
                pltpu.VMEM((SUB, chans), F32),
                pltpu.VMEM((3, rows + SUB, width), F32),
                pltpu.VMEM((rows, width), F32),
                pltpu.VMEM((rows, chans), F32),
                pltpu.VMEM((rows, chans), F32),
                pltpu.VMEM((rows // SUB * modes, chans), F32),
                pltpu.VMEM((modes * SUB, chans), F32),
                pltpu.VMEM((SUB * SUB, chans), F32),
                pltpu.VMEM((rows, width), bf16),
                pltpu.VMEM((chunks, modes, width), F32),
                pltpu.VMEM((chunks, modes, width), F32),
                pltpu.VMEM((chunks, modes, width), F32),
                pltpu.VMEM((n // 2, chunks, modes, width), F32),
                pltpu.VMEM((rows, w_out.shape[1]), F32),
                dma((3,)),
                dma,
                dma((2,)),
                dma((chunks,)),
                dma((chunks,)),
                dma((n // 2, 2, chunks)),
                dma((n // 2, chunks)),
            ],
            compiler_params=pltpu.CompilerParams(
                collective_id=0, has_side_effects=True, vmem_limit_bytes=60 * 1024 * 1024
            ),
        )(queries, keys, values, short_taps, decay.T, residue.T, skip[None, :], w_out)

    placed = (P(("rep", "seq"), None),) * 3 + (P(),) * 5
    return jax.shard_map(
        body, mesh=mesh, in_specs=placed, out_specs=P(("rep", "seq"), None), check_vma=False
    )
```

time: 132 us -> 18.7 us (0.14)
  the two profiles are of different devices: /device:TPU:0 before, /device:TPU:5 now
where the time goes in v1:
time: 18.7 us; the launch traced here: 18.5 us
  Pallas kernels  16.7 us (89%)
  local copies, waits for them, and re-layouts  1.88 us (10%)
    pallas_call x1, Pallas kernels, body(): pl.pallas_call(functools.partial(kernel, n, width), out_shape=jax.ShapeDt...  16.7 us
    unnamed x1, local copies, waits for them, and re-layouts  1.88 us

profile of v1, /device:TPU:5, one launch (start us, length us, event | category | flops | bytes accessed | tf_op | source)
XLA Modules:
  0.0 18.5 jit_solution(6749897446261495840)
XLA Ops:
  0.0 16.7 %shard_map.82 = bf16[128,2048]{1,0:T(8,128)(2,1)} custom-call(bf16[128,2048]{1,0:T(8,128)(2,1)} %q_hbm.1, bf16[128,2048]{1,0:T(8,128)(2,1)} %k_hbm.1, bf16[128,2048]{1,0:T(8,128)(2,1)} %v_hbm.1, f32[3,3,2048]{2,1,0:T(4,128)} %taps_ref.1, f32[16,2048]{1,0:T(8,128)} %bitcast.3, f32[16,2048]{1,0:T(8,128)} %bitcast.4, f32[1,2048]{1,0:T(1,128)} %bitcast.5, ...), custom_call_target="tpu_custom_call" | custom-call | tf_op jit(solution)/shard_map/pallas_call | solution.py:257
  16.7 1.9 %copy.10 = bf16[128,2048]{1,0:T(8,128)(2,1)} copy(bf16[128,2048]{1,0:T(8,128)(2,1)} %shard_map.82) | data formatting | bytes 1048576

commit v2 on v1

--- a/solution.py
+++ b/solution.py
@@ -15,9 +15,9 @@
 
 def kernel(
     n, width,
-    q_hbm, k_hbm, v_hbm, taps_ref, rates_ref, residue_ref, skip_ref, w_hbm,
+    q_hbm, k_hbm, v_hbm, taps_hbm, rates_hbm, residue_hbm, skip_hbm, w_hbm,
     out_ref,
-    q_in, k_in, v_in, w_in, tails_out, tails_in, ext, sig, q_short, partial, states,
+    q_in, k_in, v_in, taps_ref, rates_ref, residue_ref, skip_ref, w_in, tails_out, tails_in, ext, sig, q_short, partial, states,
     carry_table, tap_table, gated, ends, before, totals, earlier, total_out,
     in_sems, w_sem, tail_sems, pair_send, pair_recv, group_send, group_recv,
 ):
@@ -41,14 +41,17 @@
     lax.fori_loop(1, n, greet, 0)
     loads = [
         pltpu.make_async_copy(src, dst, in_sems.at[i])
-        for i, (src, dst) in enumerate(((q_hbm, q_in), (k_hbm, k_in), (v_hbm, v_in)))
+        for i, (src, dst) in enumerate((
+            (q_hbm, q_in), (k_hbm, k_in), (v_hbm, v_in), (rates_hbm, rates_ref),
+            (residue_hbm, residue_ref), (skip_hbm, skip_ref), (taps_hbm, taps_ref),
+        ))
     ]
     for load in loads:
         load.start()
     w_load = pltpu.make_async_copy(w_hbm, w_in, w_sem)
     w_load.start()
 
-    for load in loads:
+    for load in loads[:3]:
         load.wait()
     for i, tokens in enumerate((q_in, k_in, v_in)):
         last = tokens[rows - 16 :, :].astype(F32)
@@ -86,6 +89,9 @@
     @pl.when(odd == 0)
     def _():
         before[...] = jnp.zeros_like(before)
+
+    for load in loads[3:]:
+        load.wait()
 
     place = lax.broadcasted_iota(jnp.int32, (SUB, width), 0)
     steps = (place + 1).astype(F32)
@@ -108,6 +114,32 @@
 
     lax.fori_loop(0, chunks, tables, 0)
 
+    strip = math.gcd(rows, 16)
+
+    def mix(g, first, last):
+        cols = pl.ds(pl.multiple_of(g * width, width), width)
+        for i, tokens in enumerate((q_in, k_in, v_in)):
+            for r in range(max(first - strip, 0), last, strip):
+                ext[i, SUB + r : SUB + r + strip, :] = tokens[r : r + strip, cols].astype(F32)
+
+        def short(i, r):
+            result = taps_ref[i, 0:1, cols] * ext[i, SUB + r : SUB + r + strip, :]
+            result = result + taps_ref[i, 1:2, cols] * ext[i, SUB + r - 1 : SUB + r + strip - 1, :]
+            return result + taps_ref[i, 2:3, cols] * ext[i, SUB + r - 2 : SUB + r + strip - 2, :]
+
+        for r in range(first, last, strip):
+            mixed = (short(1, r) * short(2, r)).astype(jnp.bfloat16)
+            mixed = mixed.astype(F32)
+            for j in range(0, strip, SUB):
+                sig[(r + j) // SUB, :, cols] = mixed[j : j + SUB]
+            q_short[r : r + strip, cols] = short(0, r)
+
+    def mix_later(g, carry):
+        mix(g, strip, rows)
+        return carry
+
+    lax.fori_loop(0, chunks, mix_later, 0)
+
     @pl.when(me > 0)
     def _():
         tail_copy().wait_recv()
@@ -121,7 +153,7 @@
             def _():
                 cols = pl.ds(pl.multiple_of(g * width, width), width)
                 span = jnp.exp(-float(rows) * rates_ref[:, cols])
-                totals[g] = span * before[g] + ends[g]
+                totals[g] = (span * before[g] + ends[g]).astype(totals.dtype)
 
                 def send(target, carry):
                     for core in range(2):
@@ -130,33 +162,19 @@
 
                 lax.fori_loop(group + 1, groups, send, 0)
 
-    strip = math.gcd(rows, 16)
-
     def local(g, carry):
         cols = pl.ds(pl.multiple_of(g * width, width), width)
-        for i, tokens in enumerate((q_in, k_in, v_in)):
+        for i in range(3):
             ext[i, SUB - 2 : SUB, :] = tails_in[2 * i : 2 * i + 2, cols]
-            for r in range(0, rows, strip):
-                ext[i, SUB + r : SUB + r + strip, :] = tokens[r : r + strip, cols].astype(F32)
-
-        def short(i, r):
-            result = taps_ref[i, 0:1, cols] * ext[i, SUB + r : SUB + r + strip, :]
-            result = result + taps_ref[i, 1:2, cols] * ext[i, SUB + r - 1 : SUB + r + strip - 1, :]
-            return result + taps_ref[i, 2:3, cols] * ext[i, SUB + r - 2 : SUB + r + strip - 2, :]
-
-        for r in range(0, rows, strip):
-            mixed = (short(1, r) * short(2, r)).astype(jnp.bfloat16)
-            sig[r : r + strip, :] = mixed.astype(F32)
-            q_short[r : r + strip, cols] = short(0, r)
-
+        mix(g, 0, strip)
         fade = jnp.exp(-rates_ref[:, cols])
 
         def block(b, state):
-            states[pl.ds(pl.multiple_of(b * modes, modes), modes), cols] = state
+            states[b, :, cols] = state
             base = pl.multiple_of(b * SUB, SUB)
             acc = None
             for s in range(SUB):
-                row = sig[pl.ds(base + s, 1), :]
+                row = sig[b, s : s + 1, cols]
                 state = state * fade + row
                 term = tap_table[s * SUB : (s + 1) * SUB, cols] * row
                 acc = term if acc is None else acc + term
@@ -179,7 +197,13 @@
     combine(chunks - 1)
     w_load.wait()
     batch = 4 if blocks % 4 == 0 else 1
-    tile = math.gcd(chans, 512)
+    tile = out_ref.shape[1] // (blocks // batch)
+
+    def project(g, side, k):
+        source = pl.ds(pl.multiple_of(g * width, width), width)
+        here = pl.ds(pl.multiple_of(k * tile, tile), tile)
+        piece = jnp.dot(gated[side], w_in[source, here], preferred_element_type=F32)
+        total_out[:, here] += piece
 
     def finish(g, carry):
         cols = pl.ds(pl.multiple_of(g * width, width), width)
@@ -188,39 +212,44 @@
 
         def gather(source, state):
             group_copy(source, group, odd, g).wait_recv()
-            return state * far + earlier[source, g]
+            return state * far + earlier[source, g].astype(F32)
 
         entering = lax.fori_loop(0, group, gather, jnp.zeros((modes, width), F32))
         span = jnp.where(odd == 1, jnp.exp(-float(rows) * rates), 1.0)
         entering = span * entering + before[g]
         fade = jnp.exp(-float(SUB) * rates)
         for b in range(blocks):
-            here = slice(b * modes, (b + 1) * modes)
-            states[here, cols] = states[here, cols] + entering
+            states[b, :, cols] = states[b, :, cols] + entering
             entering = entering * fade
 
+        side = lax.rem(g, 2)
+
         def outputs(k, inner):
+            project(jnp.maximum(g - 1, 0), 1 - side, k)
             base = pl.multiple_of(k * batch * SUB, batch * SUB)
             accs = [partial[pl.ds(base + j * SUB, SUB), cols] for j in range(batch)]
             for m in range(modes):
                 table = carry_table[m * SUB : (m + 1) * SUB, cols]
                 for j in range(batch):
-                    row = states[pl.ds((k * batch + j) * modes + m, 1), cols]
+                    row = states[k * batch + j, m : m + 1, cols]
                     accs[j] = accs[j] + table * row
             long_out = jnp.concatenate(accs, axis=0).astype(jnp.bfloat16).astype(F32)
             here = pl.ds(base, batch * SUB)
-            gated[here, :] = (q_short[here, cols] * long_out).astype(jnp.bfloat16)
+            gated[side, here, :] = (q_short[here, cols] * long_out).astype(jnp.bfloat16)
             return inner
 
         lax.fori_loop(0, blocks // batch, outputs, 0)
-        for c in range(0, chans, tile):
-            piece = jnp.dot(gated[...], w_in[cols, c : c + tile], preferred_element_type=F32)
-            total_out[:, c : c + tile] += piece
-        return carry
-
+        return carry
+
+    gated[1] = jnp.zeros(gated.shape[1:], gated.dtype)
     total_out[...] = jnp.zeros_like(total_out)
     lax.fori_loop(0, chunks, finish, 0)
-    out_ref[...] = total_out[...].astype(out_ref.dtype)
+    for k in range(blocks // batch):
+        here = slice(k * tile, (k + 1) * tile)
+        piece = jnp.dot(
+            gated[(chunks - 1) % 2], w_in[chans - width :, here], preferred_element_type=F32
+        )
+        out_ref[:, here] = (total_out[:, here] + piece).astype(out_ref.dtype)
 
     @pl.when(me < n - 1)
     def _():
@@ -257,29 +286,33 @@
         return pl.pallas_call(
             functools.partial(kernel, n, width),
             out_shape=jax.ShapeDtypeStruct((rows, w_out.shape[1]), bf16),
-            in_specs=[hbm, hbm, hbm, vmem, vmem, vmem, vmem, hbm],
+            in_specs=[hbm] * 8,
             out_specs=vmem,
             scratch_shapes=[
                 pltpu.VMEM((rows, chans), bf16),
                 pltpu.VMEM((rows, chans), bf16),
                 pltpu.VMEM((rows, chans), bf16),
+                pltpu.VMEM(short_taps.shape, F32),
+                pltpu.VMEM((modes, chans), F32),
+                pltpu.VMEM((modes, chans), F32),
+                pltpu.VMEM((1, chans), F32),
                 pltpu.VMEM(w_out.shape, bf16),
                 pltpu.VMEM((SUB, chans), F32),
                 pltpu.VMEM((SUB, chans), F32),
                 pltpu.VMEM((3, rows + SUB, width), F32),
-                pltpu.VMEM((rows, width), F32),
+                pltpu.VMEM((rows // SUB, SUB, chans), F32),
                 pltpu.VMEM((rows, chans), F32),
                 pltpu.VMEM((rows, chans), F32),
-                pltpu.VMEM((rows // SUB * modes, chans), F32),
+                pltpu.VMEM((rows // SUB, modes, chans), F32),
                 pltpu.VMEM((modes * SUB, chans), F32),
                 pltpu.VMEM((SUB * SUB, chans), F32),
-                pltpu.VMEM((rows, width), bf16),
+                pltpu.VMEM((2, rows, width), bf16),
                 pltpu.VMEM((chunks, modes, width), F32),
                 pltpu.VMEM((chunks, modes, width), F32),
-                pltpu.VMEM((chunks, modes, width), F32),
-                pltpu.VMEM((n // 2, chunks, modes, width), F32),
+                pltpu.VMEM((chunks, modes, width), bf16),
+                pltpu.VMEM((n // 2, chunks, modes, width), bf16),
                 pltpu.VMEM((rows, w_out.shape[1]), F32),
-                dma((3,)),
+                dma((7,)),
                 dma,
                 dma((2,)),
                 dma((chunks,)),

time: 18.7 us -> 18.1 us (0.968)
  Pallas kernels: 16.7 us -> 16.1 us
    pallas_call x1, Pallas kernels: 16.7 us -> 16.1 us  [body(): pl.pallas_call(functools.partial(kernel, n, width), out_shape=jax.ShapeDt...]
where the time goes in v2:
time: 18.1 us; the launch traced here: 18 us
  Pallas kernels  16.1 us (89%)
  local copies, waits for them, and re-layouts  1.88 us (10%)
    pallas_call x1, Pallas kernels, body(): pl.pallas_call(functools.partial(kernel, n, width), out_shape=jax.ShapeDt...  16.1 us
    unnamed x1, local copies, waits for them, and re-layouts  1.88 us

profile of v2, /device:TPU:5, one launch (start us, length us, event | category | flops | bytes accessed | tf_op | source)
XLA Modules:
  0.0 18.0 jit_solution(4916957943317658486)
XLA Ops:
  0.0 16.1 %shard_map.82 = bf16[128,2048]{1,0:T(8,128)(2,1)} custom-call(bf16[128,2048]{1,0:T(8,128)(2,1)} %q_hbm.1, bf16[128,2048]{1,0:T(8,128)(2,1)} %k_hbm.1, bf16[128,2048]{1,0:T(8,128)(2,1)} %v_hbm.1, f32[3,3,2048]{2,1,0:T(4,128)} %taps_hbm.1, f32[16,2048]{1,0:T(8,128)} %bitcast.3, f32[16,2048]{1,0:T(8,128)} %bitcast.4, f32[1,2048]{1,0:T(1,128)} %bitcast.5, ...), custom_call_target="tpu_custom_call" | custom-call | tf_op jit(solution)/shard_map/pallas_call | solution.py:286
  16.1 1.9 %copy.10 = bf16[128,2048]{1,0:T(8,128)(2,1)} copy(bf16[128,2048]{1,0:T(8,128)(2,1)} %shard_map.82) | data formatting | bytes 1048576

commit v3 on v2

--- a/solution.py
+++ b/solution.py
@@ -49,10 +49,10 @@
     for load in loads:
         load.start()
     w_load = pltpu.make_async_copy(w_hbm, w_in, w_sem)
-    w_load.start()
 
     for load in loads[:3]:
         load.wait()
+    w_load.start()
     for i, tokens in enumerate((q_in, k_in, v_in)):
         last = tokens[rows - 16 :, :].astype(F32)
         tails_out[2 * i : 2 * i + 2, :] = last[14:16]
@@ -321,7 +321,7 @@
                 dma((n // 2, chunks)),
             ],
             compiler_params=pltpu.CompilerParams(
-                collective_id=0, has_side_effects=True, vmem_limit_bytes=60 * 1024 * 1024
+                collective_id=0, has_side_effects=True, vmem_limit_bytes=54272 * 1024
             ),
         )(queries, keys, values, short_taps, decay.T, residue.T, skip[None, :], w_out)
 

time: 18.1 us -> 19.8 us (1.094)
  local copies, waits for them, and re-layouts: 1.88 us -> 4.19 us
  Pallas kernels: 16.1 us -> 15.3 us
    unnamed x1 -> x9, local copies, waits for them, and re-layouts: 1.88 us -> 4.19 us
    pallas_call x1, Pallas kernels: 16.1 us -> 15.3 us  [body(): pl.pallas_call(functools.partial(kernel, n, width), out_shape=jax.ShapeDt...]
where the time goes in v3:
time: 19.8 us; the launch traced here: 19.5 us
  Pallas kernels  15.3 us (77%)
  local copies, waits for them, and re-layouts  4.19 us (21%)
    pallas_call x1, Pallas kernels, body(): pl.pallas_call(functools.partial(kernel, n, width), out_shape=jax.ShapeDt...  15.3 us
    unnamed x9, local copies, waits for them, and re-layouts  4.19 us

profile of v3, /device:TPU:5, one launch (start us, length us, event | category | flops | bytes accessed | tf_op | source)
XLA Modules:
  0.0 19.5 jit_solution(16311654071279600982)
XLA Ops:
  0.0 0.0 copy-start
  0.0 0.9 %copy-done = f32[2048,16]{0,1:T(8,128)S(1)} copy-done((f32[2048,16]{0,1:T(8,128)S(1)}, f32[2048,16]{0,1:T(8,128)}, u32[]{:S(2)}) %copy-start) | copy-done | bytes 131096
  0.9 0.0 copy-start.1
  0.9 0.9 %copy-done.1 = f32[2048,16]{0,1:T(8,128)S(1)} copy-done((f32[2048,16]{0,1:T(8,128)S(1)}, f32[2048,16]{0,1:T(8,128)}, u32[]{:S(2)}) %copy-start.1) | copy-done | bytes 131096
  1.8 0.0 copy-start.2
  1.8 0.9 %copy-done.2 = f32[3,3,2048]{2,1,0:T(4,128)S(1)} copy-done((f32[3,3,2048]{2,1,0:T(4,128)S(1)}, f32[3,3,2048]{2,1,0:T(4,128)}, u32[]{:S(2)}) %copy-start.2) | copy-done | bytes 73752
  2.7 0.0 copy-start.3
  2.7 0.7 %copy-done.3 = f32[2048]{0:T(1024)S(1)} copy-done((f32[2048]{0:T(1024)S(1)}, f32[2048]{0:T(1024)}, u32[]{:S(2)}) %copy-start.3) | copy-done | bytes 8216
  3.4 15.3 %shard_map.82 = bf16[128,2048]{1,0:T(8,128)(2,1)S(1)} custom-call(bf16[128,2048]{1,0:T(8,128)(2,1)} %q_hbm.1, bf16[128,2048]{1,0:T(8,128)(2,1)} %k_hbm.1, bf16[128,2048]{1,0:T(8,128)(2,1)} %v_hbm.1, f32[3,3,2048]{2,1,0:T(4,128)S(1)} %copy-done.2, f32[16,2048]{1,0:T(8,128)S(1)} %bitcast.3, f32[16,2048]{1,0:T(8,128)S(1)} %bitcast.4, f32[1,2048]{1,0:T(1,128)S(1)} %bitcast.5, ...), custom_call_target="tpu_custom_call" | custom-call | tf_op jit(solution)/shard_map/pallas_call | solution.py:286
  18.7 0.8 %copy.10 = bf16[128,2048]{1,0:T(8,128)(2,1)} copy(bf16[128,2048]{1,0:T(8,128)(2,1)S(1)} %shard_map.82) | data formatting | bytes 1048576
Async XLA Ops:
  0.0 0.9 %copy-start = (f32[2048,16]{0,1:T(8,128)S(1)}, f32[2048,16]{0,1:T(8,128)}, u32[]{:S(2)}) copy-start(f32[2048,16]{0,1:T(8,128)} %param.12) | copy-start | bytes 393220
  0.9 0.9 %copy-start.1 = (f32[2048,16]{0,1:T(8,128)S(1)}, f32[2048,16]{0,1:T(8,128)}, u32[]{:S(2)}) copy-start(f32[2048,16]{0,1:T(8,128)} %param.13) | copy-start | bytes 393220
  1.8 0.9 %copy-start.2 = (f32[3,3,2048]{2,1,0:T(4,128)S(1)}, f32[3,3,2048]{2,1,0:T(4,128)}, u32[]{:S(2)}) copy-start(f32[3,3,2048]{2,1,0:T(4,128)} %taps_hbm.1) | copy-start | bytes 221188
  2.7 0.7 %copy-start.3 = (f32[2048]{0:T(1024)S(1)}, f32[2048]{0:T(1024)}, u32[]{:S(2)}) copy-start(f32[2048]{0:T(1024)} %param.14) | copy-start | bytes 24580
